TPU v7x, 512 devices: a whole 4x8x8 slice. The times are simulated.
512 devices in a mesh: grp: 16 (over y, core), blk: 32 (over z, x).
Axes of the slice: x: 4, y: 8, z: 8, core: 2. Of those that a mesh axis runs over, the one named last changes fastest.
Arguments:
- queries: bfloat16 [16, 512, 4096], P(None, ('blk', 'grp')), may hold values from -24 to 24
- cache_keys: bfloat16 [16, 14336, 512], P('grp', 'blk'), may hold values from -24 to 24
- cache_values: bfloat16 [16, 14336, 512], P('grp', 'blk'), may hold values from -15 to 15
- new_keys: bfloat16 [16, 512, 512], P(None, ('blk', 'grp')), may hold values from -6 to 6
- new_values: bfloat16 [16, 512, 512], P(None, ('blk', 'grp')), may hold values from -15 to 15
- hits: int32 [16], P('grp'), may hold values from 1792 to 14336, as said below
- counts: int32 [16], P('grp'), may hold values from 256 to 512, as said below
- assign: int32 [16, 32], P('grp'), may hold values from 0 to 31, each once within a row
Outputs:
- attended: bfloat16 [16, 512, 4096], P(None, ('blk', 'grp'))
Inputs may be any that keep to these rules, and one draw needn't show every extreme that they name: Cached positions of request r below hits[r] are valid; in every draw some request has all 14336 valid. New tokens of request r at order counts[r] or later are padding; in every draw some request has all 512.
All inputs are finite; a program needn't handle non-finite values.
Results may differ from a plain program's by a relative error of at most 0.0085.
Values may be sent and summed in bfloat16 or wider, within the bound.
A program may use at most 128 MiB of HBM per device.

v0:
```python
import jax
import jax.numpy as jnp
from jax import lax
from jax.sharding import Mesh
from jax.sharding import PartitionSpec as P

HEAD_DIM = 128
BLK = ("blk_0", "blk_1")
BLK_GRP = ("blk_0", "blk_1", "grp")


def side_by_side(arrays, axis, split_dim, concat_dim, along):
    ends, at = ([], 0)
    for a in arrays[:-1]:
        at += a.shape[along]
        ends.append(at)
    both = jnp.concatenate(arrays, axis=along)
    return tuple(
        jnp.split(
            lax.all_to_all(both, axis, split_axis=split_dim, concat_axis=concat_dim, tiled=True),
            ends,
            axis=along,
        )
    )


def gather_axes(value, axes, dim):
    result = value
    for number in range(len(axes) - 1, -1, -1):
        result = lax.all_gather(result, axes[number], axis=dim, tiled=True)
    return result


def partial_block(queries, keys, values, allowed, kv_heads):
    row_count, full_width = queries.shape
    key_count = keys.shape[0]
    head_dim = keys.shape[1] // kv_heads
    group_size = full_width // head_dim // kv_heads
    query_heads = queries.reshape(row_count, kv_heads, group_size, head_dim)
    key_heads = keys.reshape(key_count, kv_heads, head_dim)
    scores = jnp.einsum(
        "qkgd,nkd->kgqn", query_heads, key_heads, preferred_element_type=jnp.float32
    ) * head_dim ** (-0.5)
    scores = jnp.where(allowed[None, None], scores, -1e30)
    block_max = jnp.max(scores, axis=-1)
    exp_terms = jnp.where(allowed[None, None], jnp.exp(scores - block_max[..., None]), 0.0)
    weight_sum = jnp.sum(exp_terms, axis=-1)
    prob_bf = exp_terms.astype(jnp.bfloat16)
    value_heads = values.reshape(key_count, kv_heads, head_dim)
    blended = jnp.einsum("kgqn,nkd->qkgd", prob_bf, value_heads, preferred_element_type=jnp.float32)
    floor_sum = jnp.maximum(weight_sum, 1.0).transpose(2, 0, 1)[..., None]
    blended = (blended / floor_sum).reshape(row_count, full_width).astype(jnp.bfloat16)
    maxima = block_max.transpose(2, 0, 1).reshape(row_count, -1)
    weights = weight_sum.transpose(2, 0, 1).reshape(row_count, -1)
    return (blended, maxima, weights)


def local(queries, cache_keys, cache_values, new_keys, new_values, hits, counts, assign):
    local_q, local_k, local_v = side_by_side((queries, new_keys, new_values), "grp", 0, 1, 2)
    local_q = local_q[0]
    local_k = local_k[0]
    local_v = local_v[0]
    row_count, full_width = local_q.shape
    kv_width = local_k.shape[1]
    cached = cache_keys.shape[1]
    head_count = full_width // HEAD_DIM
    kv_heads = kv_width // HEAD_DIM
    hit_limit = hits[0]
    filled = counts[0]
    block_order = assign[0]
    cycle_index = lax.axis_index(BLK)
    members = lax.axis_size(BLK)
    query_lane = jnp.arange(row_count, dtype=jnp.int32)
    cache_lane = jnp.arange(cached, dtype=jnp.int32)
    own_pos = block_order[cycle_index] * row_count + query_lane
    block_keys = jnp.concatenate([cache_keys[0], local_k], 0)
    block_values = jnp.concatenate([cache_values[0], local_v], 0)
    every_q = gather_axes(local_q, BLK, 0)
    total_rows = every_q.shape[0]
    every_lane = jnp.arange(total_rows, dtype=jnp.int32)
    every_pos = block_order[every_lane // row_count] * row_count + every_lane % row_count
    cache_ok = cycle_index * cached + cache_lane < hit_limit
    fresh_ok = (block_order[cycle_index] * row_count + query_lane)[None, :] <= every_pos[:, None]
    allowed_here = jnp.concatenate(
        [jnp.broadcast_to(cache_ok[None, :], (every_pos.shape[0], cached)), fresh_ok], 1
    )
    group_size = head_count // kv_heads
    part_count = group_size // 4
    sub_width = group_size // part_count * HEAD_DIM

    def one_slice(slot):
        kv_slot = slot // part_count
        query_slice = lax.dynamic_slice_in_dim(every_q, slot * sub_width, sub_width, 1)
        keys_here = lax.dynamic_slice_in_dim(block_keys, kv_slot * HEAD_DIM, HEAD_DIM, 1)
        values_here = lax.dynamic_slice_in_dim(block_values, kv_slot * HEAD_DIM, HEAD_DIM, 1)
        return partial_block(query_slice, keys_here, values_here, allowed_here, 1)

    slice_out, slice_max, slice_weight = lax.map(
        one_slice, jnp.arange(kv_heads * part_count, dtype=jnp.int32)
    )
    every_out = slice_out.transpose(1, 0, 2).reshape(total_rows, full_width)
    every_max = slice_max.transpose(1, 0, 2).reshape(total_rows, head_count)
    every_weight = slice_weight.transpose(1, 0, 2).reshape(total_rows, head_count)
    back_out = lax.all_to_all(every_out, BLK, split_axis=0, concat_axis=0, tiled=True)
    back_max, back_weight = side_by_side((every_max, every_weight), BLK, 0, 0, 1)
    stacked_max = back_max.reshape(members, row_count, head_count)
    stacked_weight = back_weight.reshape(members, row_count, head_count)
    highest = jnp.max(stacked_max, axis=0)
    scales = stacked_weight * jnp.exp(stacked_max - highest[None])
    total = jnp.sum(scales, axis=0)
    stacked_out = back_out.reshape(members, row_count, head_count, HEAD_DIM)
    summed = jnp.sum(scales[..., None] * stacked_out.astype(jnp.float32), axis=0)
    running = (summed.reshape(row_count, full_width), highest, total)
    summed, maxima, weights = running
    blended = (summed.reshape(row_count, head_count, -1) / weights[:, :, None]).reshape(
        row_count, full_width
    )
    blended = jnp.where((own_pos < filled)[:, None], blended, 0.0).astype(jnp.bfloat16)
    return lax.all_to_all(blended[None], "grp", split_axis=1, concat_axis=0, tiled=True)


def solution(mesh):
    finer = Mesh(mesh.devices.reshape(mesh.shape["grp"], 8, 4), ("grp", "blk_0", "blk_1"))
    in_specs = (
        P(None, BLK_GRP, None),
        P("grp", BLK, None),
        P("grp", BLK, None),
        P(None, BLK_GRP, None),
        P(None, BLK_GRP, None),
        P("grp"),
        P("grp"),
        P("grp", None),
    )
    out_specs = P(None, BLK_GRP, None)
    return jax.shard_map(local, mesh=finer, in_specs=in_specs, out_specs=out_specs, check_vma=False)
```

profile of v0, /device:TPU:1, one launch (start us, length us, event | category | flops | bytes accessed | tf_op | source)
XLA Modules:
  0.0 327.4 jit_solution(11620801276821185149)
XLA Ops:
  6.5 1.0 pad_maximum_fusion.3
  8.1 0.7 reduce.59
  8.9 18.9 %all_to_all.42 = bf16[16,2,2560]{2,1,0:T(2,128)(2,1)S(1)} all-to-all(bf16[16,2,2560]{2,1,0:T(2,128)(2,1)S(1)} %reshape.453), channel_id=1, replica_groups=mesh['grp'=16,'blk_0'=8,'blk_1'=4] {'grp'}, dimensions={0} | all-to-all | bytes 327680 | tf_op jit(solution)/shard_map/all_to_all | solution.py:20
  28.0 11.8 %all-gather = bf16[1,64,4096]{2,1,0:T(8,128)(2,1)} all-gather(bf16[1,16,4096]{2,1,0:T(8,128)(2,1)S(1)} %split.22), channel_id=2, replica_groups=mesh['grp'=16,'blk_0'=8,'blk_1'=4] {'blk_1'}, dimensions={1}, use_global_device_ids=true | all-gather | bytes 655360 | tf_op jit(solution)/shard_map/all_gather | solution.py:30
  40.5 1.9 fusion.30
  43.8 0.7 fusion.29
  44.6 4.5 %compare_select_fusion.1 = s32[512,1]{0,1:T(1,128)S(1)} fusion(s32[]{:T(128)} %bitcast.48, s32[]{:T(128)} %bitcast.49, s32[]{:T(128)} %bitcast.50, s32[]{:T(128)} %bitcast.51, s32[]{:T(128)} %bitcast.52, s32[]{:T(128)} %bitcast.54, s32[]{:T(128)} %bitcast.53), kind=kLoop, calls=%fused_computation.67 | loop fusion | flops 11776 | bytes 2076 | tf_op jit(solution)/shard_map/gather | solution.py:81
  49.1 15.3 %fusion.24 = s32[512]{0:T(512)S(1)} fusion(pred[512]{0:T(512)(128)(4,1)S(1)} %compare_reduce_fusion, pred[512]{0:T(512)(128)(4,1)S(1)} %compare_reduce_fusion.1, pred[512]{0:T(512)(128)(4,1)S(1)} %compare_reduce_fusion.2, pred[512]{0:T(512)(128)(4,1)S(1)} %compare_reduce_fusion.3, pred[512]{0:T(512)(128)(4,1)S(1)} %compare_reduce_fusion.4, ...), kind=kLoop, calls=%fused_computation.78 | loop fusion | flops 16896 | bytes 16996 | tf_op jit(solution)/shard_map/add | solution.py:81
  64.7 34.2 %all-gather.4.cloned.1.call-done = bf16[1,512,4096]{2,1,0:T(8,128)(2,1)} async-done(((bf16[1,64,4096]{2,1,0:T(8,128)(2,1)}), bf16[1,512,4096]{2,1,0:T(8,128)(2,1)}) %all-gather.4.cloned.1.call-update) | async-done | bytes 4194320 | tf_op jit(solution)/shard_map/all_gather | solution.py:30
  98.9 68.8 %while.16 = (s32[]{:T(128)}, bf16[8,512,512]{1,2,0:T(8,128)(2,1)}, f32[8,512,4]{1,2,0:T(4,128)S(1)}, f32[8,512,4]{1,2,0:T(4,128)S(1)}, s32[8]{0:T(128)S(1)}, /*i...) while((s32[]{:T(128)}, bf16[8,512,512]{1,2,0:T(8,128)(2,1)}, ...), condition=%wide.region_3.4_spmd, body=%wide.region_0.3_spmd.sunk | while | flops 499415072 | bytes 16638375 | solution.py:98
  98.9 0.6 dynamic_slice.49
  102.3 1.1 constant_dynamic-slice_fusion.3
  103.6 0.8 fusion.42
  104.4 1.0 fusion.43
  105.4 1.2 divide_convert_fusion.2
  106.6 0.8 constant_dynamic-update-slice_fusion.2
  110.9 1.1 constant_dynamic-slice_fusion.3
  112.2 0.8 fusion.42
  113.0 1.0 fusion.43
  114.0 1.2 divide_convert_fusion.2
  115.2 0.9 constant_dynamic-update-slice_fusion.2
  119.5 1.1 constant_dynamic-slice_fusion.3
  120.8 0.8 fusion.42
  121.6 1.0 fusion.43
  122.6 1.2 divide_convert_fusion.2
  123.8 0.8 constant_dynamic-update-slice_fusion.2
  128.1 1.1 constant_dynamic-slice_fusion.3
  129.4 0.8 fusion.42
  130.2 1.0 fusion.43
  131.1 1.2 divide_convert_fusion.2
  132.4 0.8 constant_dynamic-update-slice_fusion.2
  136.7 1.1 constant_dynamic-slice_fusion.3
  138.0 0.8 fusion.42
  138.8 1.0 fusion.43
  139.8 1.2 divide_convert_fusion.2
  141.0 0.8 constant_dynamic-update-slice_fusion.2
  145.3 1.1 constant_dynamic-slice_fusion.3
  146.6 0.8 fusion.42
  147.4 1.0 fusion.43
  148.4 1.2 divide_convert_fusion.2
  149.6 0.9 constant_dynamic-update-slice_fusion.2
  153.9 1.1 constant_dynamic-slice_fusion.3
  155.2 0.8 fusion.42
  156.0 1.0 fusion.43
  157.0 1.2 divide_convert_fusion.2
  158.2 0.8 constant_dynamic-update-slice_fusion.2
  162.5 1.1 constant_dynamic-slice_fusion.3
  163.8 0.8 fusion.42
  164.6 1.0 fusion.43
  165.6 1.2 divide_convert_fusion.2
  166.8 0.9 constant_dynamic-update-slice_fusion.2
  168.9 0.8 reshape.455
  169.7 6.7 %all-to-all-start.1 = ((f32[32,1,1024]{2,1,0:T(1,128)}), f32[32,1,1024]{2,1,0:T(1,128)S(1)}, u32[]{:S(2)}, u32[]{:S(2)}) async-start(f32[32,1,1024]{2,1,0:T(1,128)} %reshape.455), calls=%async_computation.1 | async-start | bytes 262144 | tf_op jit(solution)/shard_map/all_to_all | solution.py:20
  176.4 8.0 %copy.28 = bf16[512,8,512]{2,1,0:T(8,128)(2,1)} copy(bf16[512,8,512]{0,2,1:T(8,128)(2,1)} %bitcast.163) | data formatting | bytes 8388608 | tf_op jit(solution)/shard_map/transpose | solution.py:101
  184.4 7.4 %all_to_all.34 = bf16[32,16,4096]{2,1,0:T(8,128)(2,1)} reshape(bf16[512,8,512]{2,1,0:T(8,128)(2,1)} %copy.28) | data formatting | bytes 8388608 | tf_op jit(solution)/shard_map/all_to_all | solution.py:104
  191.8 9.5 %all-to-all-start.2 = ((bf16[32,16,4096]{2,1,0:T(8,128)(2,1)}), bf16[32,16,4096]{2,1,0:T(8,128)(2,1)}, u32[]{:S(2)}, u32[]{:S(2)}) async-start(bf16[32,16,4096]{2,1,0:T(8,128)(2,1)} %all_to_all.34), calls=%async_computation.2 | async-start | bytes 8388608 | tf_op jit(solution)/shard_map/all_to_all | solution.py:104
  202.5 0.9 reduce.60
  203.9 4.6 %mul.70 = f32[32,16,32,128]{3,2,1,0:T(8,128)} broadcast(f32[32,16,32]{2,1,0:T(8,128)S(1)} %exponential_multiply_fusion), dimensions={0,1,2} | broadcast | bytes 8454144 | tf_op jit(solution)/shard_map/mul | solution.py:112
  208.5 9.4 %mul.71 = f32[32,16,4096]{2,1,0:T(8,128)} reshape(f32[32,16,32,128]{3,2,1,0:T(8,128)} %mul.70) | data formatting | bytes 16777216 | tf_op jit(solution)/shard_map/mul | solution.py:112
  217.8 75.7 %all-to-all-done.2 = bf16[32,16,4096]{2,1,0:T(8,128)(2,1)} async-done(((bf16[32,16,4096]{2,1,0:T(8,128)(2,1)}), bf16[32,16,4096]{2,1,0:T(8,128)(2,1)}, u32[]{:S(2)}, u32[]{:S(2)}) %all-to-all-start.2) | async-done | bytes 4194336 | tf_op jit(solution)/shard_map/all_to_all | solution.py:104
  293.5 5.7 %multiply_reduce_fusion = f32[16,4096]{1,0:T(8,128)S(1)} fusion(f32[32,16,4096]{2,1,0:T(8,128)} %mul.71, bf16[32,16,4096]{2,1,0:T(8,128)(2,1)} %all-to-all-done.2), kind=kLoop, calls=%fused_computation.26 | loop fusion | flops 6225920 | bytes 12845056 | tf_op jit(solution)/shard_map/reduce_sum | solution.py:112
  299.7 1.4 reduce.61
  301.2 18.4 %all_to_all.43 = bf16[16,2,2048]{2,1,0:T(2,128)(2,1)S(1)} all-to-all(bf16[16,2,2048]{2,1,0:T(2,128)(2,1)S(1)} %reshape.457), channel_id=1, replica_groups=mesh['grp'=16,'blk_0'=8,'blk_1'=4] {'grp'}, dimensions={0} | all-to-all | bytes 262144 | tf_op jit(solution)/shard_map/all_to_all | solution.py:119
  319.7 0.8 copy.36
  (97 shorter events, 10.5 us)
Async XLA Ops:
  6.5 37.3 %copy-start = (s32[1,32]{1,0:T(1,128)S(1)}, s32[1,32]{1,0:T(1,128)}, u32[]{:S(2)}) copy-start(s32[1,32]{1,0:T(1,128)} %param.17) | copy-start | bytes 388
  6.5 58.1 %copy-start.1 = (bf16[1,448,512]{2,1,0:T(8,128)(2,1)S(1)}, bf16[1,448,512]{2,1,0:T(8,128)(2,1)}, u32[]{:S(2)}) copy-start(bf16[1,448,512]{2,1,0:T(8,128)(2,1)} %param.12) | copy-start | bytes 1376260
  6.5 58.1 %copy-start.2 = (bf16[1,448,512]{2,1,0:T(8,128)(2,1)S(1)}, bf16[1,448,512]{2,1,0:T(8,128)(2,1)}, u32[]{:S(2)}) copy-start(bf16[1,448,512]{2,1,0:T(8,128)(2,1)} %param.11) | copy-start | bytes 1376260
  6.5 92.4 %all-gather.4.cloned.1.call-start = ((), (), s32[]{:S(2)}) async-start(), calls=%async_computation.4 | async-start | bytes 4718592 | tf_op jit(solution)/shard_map/all_gather | solution.py:30
  169.7 22.1 %all-to-all-start.1 = ((f32[32,1,1024]{2,1,0:T(1,128)}), f32[32,1,1024]{2,1,0:T(1,128)S(1)}, u32[]{:S(2)}, u32[]{:S(2)}) async-start(f32[32,1,1024]{2,1,0:T(1,128)} %reshape.455), calls=%async_computation.1 | async-start | bytes 262144 | tf_op jit(solution)/shard_map/all_to_all | solution.py:20
  191.8 101.7 %all-to-all-start.2 = ((bf16[32,16,4096]{2,1,0:T(8,128)(2,1)}), bf16[32,16,4096]{2,1,0:T(8,128)(2,1)}, u32[]{:S(2)}, u32[]{:S(2)}) async-start(bf16[32,16,4096]{2,1,0:T(8,128)(2,1)} %all_to_all.34), calls=%async_computation.2 | async-start | bytes 8388608 | tf_op jit(solution)/shard_map/all_to_all | solution.py:104
Sparse Core Ops, SparseCore 0:
  39.9 58.9 all-gather.3
where the time goes:
time: 329 us; the launch traced here: 327 us
  waiting for transfers between devices  110 us (33%)
  local copies, waits for them, and re-layouts  58.3 us (18%)
  blocking collectives  49.1 us (15%)
  other arithmetic  39 us (12%)
  loops' own time  23.2 us (7%)
  starting transfers between devices  16.2 us (5%)
  matrix products  16.2 us (5%)
  between operations  15.5 us (5%)
    all_to_all x1, waiting for transfers between devices, local(): lax.all_to_all(every_out, BLK, split_axis=0, concat_axis=0, tiled=True)  75.7 us
    all_gather x1, waiting for transfers between devices, gather_axes(): result = lax.all_gather(result, axes[number], axis=dim, tiled=True)  34.2 us
    another operation x1, loops' own time, local(): lax.map(one_slice, jnp.arange(kv_heads * part_count, dtype=jnp.int32))  23.2 us
    all_to_all x1, blocking collectives, side_by_side(): lax.all_to_all(both, axis, split_axis=split_dim, concat_axis=concat_dim,...  18.9 us
    all_to_all x1, blocking collectives, local(): lax.all_to_all(blended[None], 'grp', split_axis=1, concat_axis=0, tiled=T...  18.4 us
    add x1, other arithmetic, local(): block_order[every_lane // row_count] * row_count + every_lane % row_count  15.3 us
    mul x2, local copies, waits for them, and re-layouts, local(): scales[..., None] * stacked_out.astype(jnp.float32)  14 us
    all_gather x1, blocking collectives, gather_axes(): result = lax.all_gather(result, axes[number], axis=dim, tiled=True)  11.8 us
  transfers between devices with their start and end apart: 3, of which 2 were waited for; matrix products, arithmetic and copies ran while one was open for 14% of the time, Pallas kernels for 0%

commit v1 on v0

v1 whole, which is shorter than its diff:
```python
import functools

import jax
import jax.numpy as jnp
from jax import lax
from jax.experimental import pallas as pl
from jax.experimental.pallas import tpu as pltpu
from jax.sharding import Mesh
from jax.sharding import PartitionSpec as P

HEAD_DIM = 128
GROUP = 8
BLK = ("blk_0", "blk_1")
BLK_GRP = ("blk_0", "blk_1", "grp")
NEG = -1e30
TO_LOG2 = HEAD_DIM**-0.5 * 1.4426950408889634


def kernel(
    G, NZ, NX, C,
    q_in, kv_in, ck, cv, hits, counts, assign,
    out,
    qy, kvy, Q, K, VA, kvn, KN, VN, bias, OP, LP, OR, LR, W, res, OX,
    loc, ys, yr, xs, xr, cs, cr, ags, agr, os_, or_, fs, fr, ts, tr,
):
    g, z, x = lax.axis_index("grp"), lax.axis_index("blk_0"), lax.axis_index("blk_1")
    T = NX * G
    GR = G * GROUP
    H = NZ // 2
    PN = KN.shape[0]

    def remote(src, dst, ssem, rsem, **where):
        return pltpu.make_async_remote_copy(
            src_ref=src, dst_ref=dst, send_sem=ssem, recv_sem=rsem,
            device_id=where, device_id_type=pl.DeviceIdType.MESH,
        )

    def each(n, fn):
        def body(i, carry):
            fn(i)
            return carry
        lax.fori_loop(1, n, body, 0)

    barrier = pltpu.get_barrier_semaphore()

    def greet(axis, me, n):
        each(n, lambda i: pl.semaphore_signal(
            barrier, 1, device_id={axis: lax.rem(me + i, n)},
            device_id_type=pl.DeviceIdType.MESH))

    greet("grp", g, G)
    greet("blk_1", x, NX)
    greet("blk_0", z, NZ)

    own_lane = pl.ds(pl.multiple_of(x * HEAD_DIM, HEAD_DIM), HEAD_DIM)
    own_rows = pl.ds(pl.multiple_of(x * C, C), C)
    l_q = pltpu.make_async_copy(q_in.at[g], qy.at[g], loc.at[0])
    l_kv = pltpu.make_async_copy(kv_in.at[g], kvy.at[g], loc.at[1])
    l_k = pltpu.make_async_copy(ck.at[:, own_lane], K.at[own_rows], loc.at[2])
    l_v = pltpu.make_async_copy(cv.at[:, own_lane], VA.at[own_rows, pl.ds(0, HEAD_DIM)], loc.at[3])
    for c in (l_q, l_kv, l_k, l_v):
        c.start()

    VA[:, HEAD_DIM:] = jnp.ones((NX * C, HEAD_DIM), jnp.bfloat16)
    KN[...] = jnp.zeros((PN, HEAD_DIM), jnp.bfloat16)
    VN[:, :HEAD_DIM] = jnp.zeros((PN, HEAD_DIM), jnp.bfloat16)
    VN[:, HEAD_DIM:] = jnp.ones((PN, HEAD_DIM), jnp.bfloat16)
    limit = hits[0] - z * (NX * C)
    col = lax.broadcasted_iota(jnp.int32, (1, NX * C), 1)
    bias[...] = jnp.where(col < limit, 0.0, NEG).astype(jnp.float32)

    pl.semaphore_wait(barrier, (G - 1) + (NX - 1) + (NZ - 1))

    def y_q(i):
        p = lax.rem(g + i, G)
        return remote(q_in.at[p], qy.at[g], ys.at[0, p], yr.at[0, g], grp=p)

    def y_kv(i):
        p = lax.rem(g + i, G)
        return remote(kv_in.at[p], kvy.at[g], ys.at[1, p], yr.at[1, g], grp=p)

    each(G, lambda i: y_q(i).start())
    each(G, lambda i: y_kv(i).start())

    def x_k(i):
        p = lax.rem(x + i, NX)
        lane = pl.ds(pl.multiple_of(p * HEAD_DIM, HEAD_DIM), HEAD_DIM)
        return remote(ck.at[:, lane], K.at[own_rows], cs.at[0, p], cr.at[0, x], blk_1=p)

    def x_v(i):
        p = lax.rem(x + i, NX)
        lane = pl.ds(pl.multiple_of(p * HEAD_DIM, HEAD_DIM), HEAD_DIM)
        return remote(cv.at[:, lane], VA.at[own_rows, pl.ds(0, HEAD_DIM)], cs.at[1, p], cr.at[1, x], blk_1=p)

    l_q.wait()
    l_kv.wait()

    def y_wait(i):
        p = lax.rem(g + i, G)
        remote(q_in.at[p], qy.at[p], ys.at[0, p], yr.at[0, p], grp=p).wait_recv()
        remote(kv_in.at[p], kvy.at[p], ys.at[1, p], yr.at[1, p], grp=p).wait_recv()

    each(NX, lambda i: x_k(i).start())
    each(NX, lambda i: x_v(i).start())
    each(G, y_wait)

    def rows_of(sub):
        return pl.ds(pl.multiple_of(sub * G, G), G)

    def q_sub(zz, sub):
        return Q.at[zz, rows_of(sub)]

    def x_q(i):
        p = lax.rem(x + i, NX)
        return remote(qy.at[:, p], q_sub(z, x), xs.at[0, p], xr.at[0, x], blk_1=p)

    def x_kv(i):
        p = lax.rem(x + i, NX)
        return remote(kvy.at[:, p], kvn.at[rows_of(x)], xs.at[1, p], xr.at[1, x], blk_1=p)

    each(NX, lambda i: x_q(i).start())
    each(NX, lambda i: x_kv(i).start())

    def ag(way, step, sub, src=None):
        to = lax.rem(z + (1 if way == 0 else NZ - 1), NZ)
        held = lax.rem(z + ((NZ - step + 1) if way == 0 else (step - 1)), NZ)
        if src is None:
            src = q_sub(held, sub)
        return remote(src, q_sub(held, sub), ags.at[way, step - 1, sub], agr.at[way, step - 1, sub], blk_0=to)

    def ag_in(way, step, sub):
        to = lax.rem(z + (1 if way == 0 else NZ - 1), NZ)
        held = lax.rem(z + ((NZ - step) if way == 0 else step), NZ)
        return remote(q_sub(held, sub), q_sub(held, sub), ags.at[way, step - 1, sub], agr.at[way, step - 1, sub], blk_0=to)

    for way in (0, 1):
        ag(way, 1, x, src=qy.at[:, x]).start()
    Q[z, rows_of(x)] = qy[:, x]
    kvn[rows_of(x)] = kvy[:, x]

    def first_ring(i):
        p = lax.rem(x + i, NX)
        remote(qy.at[:, p], q_sub(z, p), xs.at[0, p], xr.at[0, p], blk_1=p).wait_recv()
        for way in (0, 1):
            ag(way, 1, p).start()

    each(NX, first_ring)

    def kv_wait(i):
        p = lax.rem(x + i, NX)
        remote(kvy.at[:, p], kvn.at[rows_of(p)], xs.at[1, p], xr.at[1, p], blk_1=p).wait_recv()

    each(NX, kv_wait)
    KN[0:T] = kvn[:, 0, :]
    VN[0:T, 0:HEAD_DIM] = kvn[:, 1, :]

    def cache_wait(i):
        p = lax.rem(x + i, NX)
        rows = pl.ds(pl.multiple_of(p * C, C), C)
        remote(ck.at[:, own_lane], K.at[rows], cs.at[0, p], cr.at[0, p], blk_1=p).wait_recv()
        remote(cv.at[:, own_lane], VA.at[rows, pl.ds(0, HEAD_DIM)], cs.at[1, p], cr.at[1, p], blk_1=p).wait_recv()

    l_k.wait()
    l_v.wait()
    each(NX, cache_wait)

    R = T * GROUP
    eye = lax.broadcasted_iota(jnp.int32, (GR, GR), 0) == lax.broadcasted_iota(jnp.int32, (GR, GR), 1)

    def position(token, block):
        pos = jnp.full(token.shape, 1 << 20, jnp.int32)
        for s in range(NX):
            here = (token >= s * G) & (token < (s + 1) * G)
            pos = jnp.where(here, assign[block * NX + s] * G + (token - s * G), pos)
        return pos

    def send_out(c):
        return (
            remote(OP.at[c], OR.at[z], os_.at[0, c], or_.at[0, z], blk_0=c),
            remote(LP.at[c], LR.at[z], os_.at[1, c], or_.at[1, z], blk_0=c),
        )

    def chunk(j, carry):
        step = (j + 1) // 2

        @pl.when(lax.rem(j, 2) == 1)
        def _():
            for sub in range(NX):
                for way in (0, 1):
                    mine = (sub < NX // 2) if way == 0 else (sub >= NX // 2)

                    def arrive(way=way, sub=sub):
                        ag_in(way, step, sub).wait_recv()

                    def onward(way=way, sub=sub):
                        ag(way, step + 1, sub).start()

                    if mine:
                        arrive()
                        pl.when(step < H)(onward)
                    else:
                        pl.when(step < H)(arrive)
                        pl.when(step < H - 1)(onward)

        c = lax.rem(jnp.where(lax.rem(j, 2) == 1, z + NZ - step, z + step), NZ)
        q = Q[c].reshape(R, HEAD_DIM)
        dn = (((1,), (1,)), ((), ()))
        s1 = lax.dot_general(q, K[...], dn, preferred_element_type=jnp.float32) + bias[...]
        s2 = lax.dot_general(q, KN[...], dn, preferred_element_type=jnp.float32)
        pt = position(lax.broadcasted_iota(jnp.int32, (R, 1), 0) // GROUP, c)
        pu = position(lax.broadcasted_iota(jnp.int32, (1, PN), 1), z)
        s2 = jnp.where(pu <= pt, s2, NEG)
        top = jnp.maximum(jnp.max(s1, axis=1, keepdims=True), jnp.max(s2, axis=1, keepdims=True))
        p1 = jnp.exp2((s1 - top) * TO_LOG2).astype(jnp.bfloat16)
        p2 = jnp.exp2((s2 - top) * TO_LOG2).astype(jnp.bfloat16)
        both = jnp.dot(p1, VA[...], preferred_element_type=jnp.float32)
        both = both + jnp.dot(p2, VN[...], preferred_element_type=jnp.float32)
        weight = both[:, HEAD_DIM:]
        OP[c] = (both[:, :HEAD_DIM] / weight).astype(jnp.bfloat16).reshape(T, GROUP, HEAD_DIM)
        level = (top * TO_LOG2 + jnp.log2(weight))[:, :GR]
        LP[c] = jnp.sum(jnp.where(eye[None], level.reshape(NX, GR, GR), 0.0), axis=1)

        @pl.when(j == 0)
        def _():
            OR[z] = OP[z]
            LR[z] = LP[z]

        @pl.when(j > 0)
        def _():
            for copy in send_out(c):
                copy.start()

        return carry

    lax.fori_loop(0, NZ, chunk, 0)

    def part_wait(i):
        b = lax.rem(z + i, NZ)
        remote(OP.at[b], OR.at[b], os_.at[0, b], or_.at[0, b], blk_0=b).wait_recv()
        remote(LP.at[b], LR.at[b], os_.at[1, b], or_.at[1, b], blk_0=b).wait_recv()

    each(NZ, part_wait)
    levels = LR[...]
    share = jnp.exp2(levels - jnp.max(levels, axis=0, keepdims=True))
    share = share / jnp.sum(share, axis=0, keepdims=True)
    slot = lax.broadcasted_iota(jnp.int32, (NX, GR), 0) * G + lax.broadcasted_iota(jnp.int32, (NX, GR), 1) // GROUP
    W[...] = jnp.where((position(slot, z) < counts[0])[None], share, 0.0)

    def x_out(p):
        return remote(res.at[rows_of(p)], OX.at[:, x], fs.at[p], fr.at[x], blk_1=p)

    def merge(i, carry):
        p = lax.rem(x + i, NX)
        total = jnp.zeros((GR, HEAD_DIM), jnp.float32)
        for b in range(NZ):
            w = jnp.sum(jnp.where(eye, W[b, pl.ds(p, 1), :], 0.0), axis=1, keepdims=True)
            total = total + w * OR[b, rows_of(p)].reshape(GR, HEAD_DIM).astype(jnp.float32)
        res[rows_of(p)] = total.astype(jnp.bfloat16).reshape(G, GROUP, HEAD_DIM)

        @pl.when(i < NX)
        def _():
            x_out(p).start()

        return carry

    lax.fori_loop(1, NX + 1, merge, 0)
    OX[:, x] = res[rows_of(x)]

    def x_out_wait(i):
        p = lax.rem(x + i, NX)
        remote(res.at[rows_of(p)], OX.at[:, p], fs.at[p], fr.at[p], blk_1=p).wait_recv()

    each(NX, x_out_wait)

    def y_out(i):
        p = lax.rem(g + i, G)
        return remote(OX.at[p], out.at[g], ts.at[p], tr.at[g], grp=p)

    each(G, lambda i: y_out(i).start())
    l_o = pltpu.make_async_copy(OX.at[g], out.at[g], loc.at[0])
    l_o.start()

    def y_out_wait(i):
        p = lax.rem(g + i, G)
        remote(OX.at[p], out.at[p], ts.at[p], tr.at[p], grp=p).wait_recv()

    each(G, y_out_wait)
    l_o.wait()

    each(G, lambda i: y_q(i).wait_send())
    each(G, lambda i: y_kv(i).wait_send())
    each(G, lambda i: y_out(i).wait_send())
    each(NX, lambda i: x_k(i).wait_send())
    each(NX, lambda i: x_v(i).wait_send())
    each(NX, lambda i: x_q(i).wait_send())
    each(NX, lambda i: x_kv(i).wait_send())
    each(NX, lambda i: x_out(lax.rem(x + i, NX)).wait_send())

    def part_sent(i):
        for copy in send_out(lax.rem(z + i, NZ)):
            copy.wait_send()

    each(NZ, part_sent)
    for way in (0, 1):
        for step in range(1, H + 1):
            for sub in range(NX):
                if step < H or ((sub < NX // 2) == (way == 0)):
                    ag(way, step, sub).wait_send()


def local(queries, cache_keys, cache_values, new_keys, new_values, hits, counts, assign):
    NZ, NX, G = lax.axis_size("blk_0"), lax.axis_size("blk_1"), lax.axis_size("grp")
    C = cache_keys.shape[1]
    T = NX * G
    PN = max(T, 128)
    N = NX * C
    q_in = queries.reshape(G, NX * GROUP, HEAD_DIM).reshape(G, NX, GROUP, HEAD_DIM)
    kv_in = jnp.stack(
        [new_keys.reshape(G, NX, HEAD_DIM), new_values.reshape(G, NX, HEAD_DIM)], axis=2
    )
    anywhere = pl.BlockSpec(memory_space=pl.ANY)
    smem = pl.BlockSpec(memory_space=pltpu.SMEM)
    bf, f32 = jnp.bfloat16, jnp.float32
    dma = pltpu.SemaphoreType.DMA
    made = pl.pallas_call(
        functools.partial(kernel, G, NZ, NX, C),
        out_shape=jax.ShapeDtypeStruct((G, NX, GROUP, HEAD_DIM), bf),
        in_specs=[anywhere] * 4 + [smem] * 3,
        out_specs=anywhere,
        scratch_shapes=[
            pltpu.VMEM((G, NX, GROUP, HEAD_DIM), bf),
            pltpu.VMEM((G, NX, 2, HEAD_DIM), bf),
            pltpu.VMEM((NZ, T, GROUP, HEAD_DIM), bf),
            pltpu.VMEM((N, HEAD_DIM), bf),
            pltpu.VMEM((N, 2 * HEAD_DIM), bf),
            pltpu.VMEM((T, 2, HEAD_DIM), bf),
            pltpu.VMEM((PN, HEAD_DIM), bf),
            pltpu.VMEM((PN, 2 * HEAD_DIM), bf),
            pltpu.VMEM((1, N), f32),
            pltpu.VMEM((NZ, T, GROUP, HEAD_DIM), bf),
            pltpu.VMEM((NZ, NX, G * GROUP), f32),
            pltpu.VMEM((NZ, T, GROUP, HEAD_DIM), bf),
            pltpu.VMEM((NZ, NX, G * GROUP), f32),
            pltpu.VMEM((NZ, NX, G * GROUP), f32),
            pltpu.VMEM((T, GROUP, HEAD_DIM), bf),
            pltpu.VMEM((G, NX, GROUP, HEAD_DIM), bf),
            dma((4,)),
            dma((2, G)), dma((2, G)),
            dma((2, NX)), dma((2, NX)),
            dma((2, NX)), dma((2, NX)),
            dma((2, NZ // 2, NX)), dma((2, NZ // 2, NX)),
            dma((2, NZ)), dma((2, NZ)),
            dma((NX,)), dma((NX,)),
            dma((G,)), dma((G,)),
        ],
        compiler_params=pltpu.CompilerParams(
            collective_id=0, has_side_effects=True, vmem_limit_bytes=56 * 1024 * 1024
        ),
        name="attend",
    )(q_in, kv_in, cache_keys[0], cache_values[0], hits, counts, assign[0])
    return made.reshape(G, 1, NX * GROUP * HEAD_DIM)


def solution(mesh):
    finer = Mesh(mesh.devices.reshape(mesh.shape["grp"], 8, 4), ("grp", "blk_0", "blk_1"))
    in_specs = (
        P(None, BLK_GRP, None),
        P("grp", BLK, None),
        P("grp", BLK, None),
        P(None, BLK_GRP, None),
        P(None, BLK_GRP, None),
        P("grp"),
        P("grp"),
        P("grp", None),
    )
    out_specs = P(None, BLK_GRP, None)
    return jax.shard_map(local, mesh=finer, in_specs=in_specs, out_specs=out_specs, check_vma=False)
```

time: 329 us -> 87.1 us (0.26)
  waiting for transfers between devices: 110 us -> 0 us
  Pallas kernels: 0 us -> 81 us
  local copies, waits for them, and re-layouts: 58.3 us -> 3.76 us
  blocking collectives: 49.1 us -> 0 us
  other arithmetic: 39 us -> 0.68 us
  loops' own time: 23.2 us -> 0 us
  matrix products: 16.2 us -> 0 us
  starting transfers between devices: 16.2 us -> 0 us
  between operations: 15.5 us -> 1.35 us
    pallas_call x0 -> x1, Pallas kernels: none -> 81 us  [local(): pl.pallas_call(functools.partial(kernel, G, NZ, NX, C), out_shape=jax.Sha...]
    all_to_all x2 -> x0, waiting for transfers between devices: 75.7 us -> none  [the longest x1 75.7 us: local(): lax.all_to_all(every_out, BLK, split_axis=0, concat_axis=0, tiled=True)]
    all_to_all x2 -> x0, blocking collectives: 37.3 us -> none  [the longest x1 18.9 us: side_by_side(): lax.all_to_all(both, axis, split_axis=split_dim, concat_axis=concat_dim,...]
    all_gather x1 -> x0, waiting for transfers between devices: 34.2 us -> none  [gather_axes(): result = lax.all_gather(result, axes[number], axis=dim, tiled=True)]
    another operation x1 -> x0, loops' own time: 23.2 us -> none  [local(): lax.map(one_slice, jnp.arange(kv_heads * part_count, dtype=jnp.int32))]
    all_to_all x2 -> x0, starting transfers between devices: 16.2 us -> none  [the longest x1 9.53 us: local(): lax.all_to_all(every_out, BLK, split_axis=0, concat_axis=0, tiled=True)]
    dot_general x16 -> x0, matrix products: 16.2 us -> none  [the longest x8 9.68 us: partial_block(): jnp.einsum('kgqn,nkd->qkgd', prob_bf, value_heads, preferred_element_type...]
    add x2 -> x0, other arithmetic: 15.3 us -> none  [the longest x1 15.3 us: local(): block_order[every_lane // row_count] * row_count + every_lane % row_count]
  transfers between devices with their start and end apart: 3 -> 0, of which waited for: 2 -> 0; matrix products, arithmetic and copies ran while one was open for 14% -> 0% of each run, Pallas kernels for 0% -> 0%
where the time goes in v1:
time: 87.1 us; the launch traced here: 86.8 us
  Pallas kernels  81 us (93%)
  local copies, waits for them, and re-layouts  3.76 us (4%)
  between operations  1.35 us (2%)
    pallas_call x1, Pallas kernels, local(): pl.pallas_call(functools.partial(kernel, G, NZ, NX, C), out_shape=jax.Sha...  81 us

profile of v1, /device:TPU:1, one launch (start us, length us, event | category | flops | bytes accessed | tf_op | source)
XLA Modules:
  0.0 86.8 jit_solution(6063856226293397770)
XLA Ops:
  0.0 0.0 copy-start
  1.3 0.7 stack_reshape.8
  2.1 0.7 stack_reshape.9
  2.8 0.7 pad_maximum_fusion.kv_in
  3.5 0.0 copy-done
  3.5 0.7 copy.11
  4.2 81.0 %attend.1 = bf16[16,4,8,128]{3,2,1,0:T(8,128)(2,1)} custom-call(bf16[16,4,8,128]{3,2,1,0:T(8,128)(2,1)} %bitcast.14, bf16[16,4,2,128]{3,2,1,0:T(2,128)(2,1)} %pad_maximum_fusion.kv_in, bf16[448,512]{1,0:T(8,128)(2,1)} %bitcast.15, bf16[448,512]{1,0:T(8,128)(2,1)} %bitcast.16, s32[1]{0:T(128)S(6)} %copy.12.hits, s32[1]{0:T(128)S(6)} %copy.13.counts, s32[32]{0:T(128)} %bitcast.18), custom_call_target="tpu_custom_call" | custom-call | tf_op jit(solution)/shard_map/attend/pallas_call | solution.py:325
  85.2 1.6 %reshape.3 = bf16[16,1,4096]{2,0,1:T(8,128)(2,1)} reshape(bf16[16,4,8,128]{3,2,1,0:T(8,128)(2,1)} %attend.1) | data formatting | bytes 262144 | tf_op jit(solution)/shard_map/reshape | solution.py:361
Async XLA Ops:
  0.0 3.5 %copy-start = (bf16[16,1,4096]{2,0,1:T(8,128)(2,1)S(1)}, bf16[16,1,4096]{2,0,1:T(8,128)(2,1)}, u32[]{:S(2)}) copy-start(bf16[16,1,4096]{2,0,1:T(8,128)(2,1)} %param.8) | copy-start | bytes 393220

commit v2 on v0

v2 whole, which is shorter than its diff:
```python
import functools

import jax
import jax.numpy as jnp
from jax import lax
from jax.experimental import pallas as pl
from jax.experimental.pallas import tpu as pltpu
from jax.sharding import Mesh
from jax.sharding import PartitionSpec as P

HEAD_DIM = 128
GROUP = 8
ONES = 16
BLK = ("blk_0", "blk_1")
BLK_GRP = ("blk_0", "blk_1", "grp")
NEG = -1e30
LOWEST = -3e38
TO_LOG2 = HEAD_DIM**-0.5 * 1.4426950408889634


def kernel(
    G, NZ, NX, C,
    q_hbm, nk_hbm, nv_hbm, ck, cv, hits_hbm, counts_hbm, assign_hbm,
    out,
    hits, counts, assign, q2, nk2, nv2, wide, q3, kvf, kv3, Q, KA, V, VT, kvn, S0, S1, M0, M1,
    SB, RB, SL, RL, res, out3, size,
    loc, sent_sem, q_sem, n_sem, cache_sem, ring_sem, part_sem, o_sem,
):
    g, z, x = lax.axis_index("grp"), lax.axis_index("blk_0"), lax.axis_index("blk_1")
    T = NX * G
    GR = G * GROUP
    HX = NX // 2
    HR = HX * GR
    N1 = NX * C
    NK = KA.shape[0]
    PN = NK - N1
    HEADS = NX * GROUP
    Y = G // 2
    H = NZ // 2
    f32, bf = jnp.float32, jnp.bfloat16

    def remote(src, dst, ssem, rsem, **where):
        return pltpu.make_async_remote_copy(
            src_ref=src, dst_ref=dst, send_sem=ssem, recv_sem=rsem,
            device_id=where, device_id_type=pl.DeviceIdType.MESH,
        )

    def loop(start, n, fn):
        def body(i, carry):
            fn(i)
            return carry
        lax.fori_loop(start, n, body, 0)

    def peer(i):
        k = i // 2
        far = jnp.where(k == 0, Y // 2, (Y - k) // 2)
        step = jnp.where(lax.rem(k, 2) == 1, far, Y - far)
        return lax.rem(g // 2 + step, Y) * 2 + lax.rem(g + 1 + i, 2)

    turns = [lax.rem(x + 1 + j, NX) for j in range(NX)]

    def others(fn):
        def one(i):
            p = peer(i)
            for t in turns:
                fn(p, t)
        loop(0, G - 1, one)
        for t in turns[:-1]:
            fn(g, t)

    barrier = pltpu.get_barrier_semaphore()

    def greet(**where):
        pl.semaphore_signal(barrier, 1, device_id=where, device_id_type=pl.DeviceIdType.MESH)

    others(lambda p, t: greet(grp=p, blk_1=t))
    after, before = lax.rem(z + 1, NZ), lax.rem(z + NZ - 1, NZ)
    greet(blk_0=after)
    greet(blk_0=before)
    greet(blk_0=lax.rem(z + H - 1, NZ))
    greet(blk_0=lax.rem(z + NZ - H + 1, NZ))

    own_lane = pl.ds(pl.multiple_of(x * HEAD_DIM, HEAD_DIM), HEAD_DIM)
    low = pl.ds(0, HEAD_DIM)

    def rows_from(p):
        return pl.ds(pl.multiple_of(p * C, C), C)

    ins = [
        pltpu.make_async_copy(q_hbm, q2, loc.at[0]),
        pltpu.make_async_copy(nk_hbm, nk2, loc.at[1]),
        pltpu.make_async_copy(nv_hbm, nv2, loc.at[2]),
        pltpu.make_async_copy(ck.at[:, own_lane], KA.at[rows_from(x), low], loc.at[3]),
        pltpu.make_async_copy(cv.at[:, own_lane], V.at[rows_from(x)], loc.at[4]),
        pltpu.make_async_copy(hits_hbm, hits, loc.at[5]),
        pltpu.make_async_copy(counts_hbm, counts, loc.at[6]),
        pltpu.make_async_copy(assign_hbm, assign, loc.at[7]),
    ]
    for c in ins:
        c.start()

    ins[0].wait()
    for h in range(HEADS):
        wide[pl.ds(h, G, stride=HEADS), :] = q2[:, h * HEAD_DIM : (h + 1) * HEAD_DIM].astype(f32)
    q3[...] = wide[...].astype(bf).reshape(G, NX, GROUP, HEAD_DIM)
    ins[1].wait()
    ins[2].wait()
    for h in range(NX):
        cut = slice(h * HEAD_DIM, (h + 1) * HEAD_DIM)
        kvf[pl.ds(2 * h, G, stride=2 * NX), :] = nk2[:, cut].astype(f32)
        kvf[pl.ds(2 * h + 1, G, stride=2 * NX), :] = nv2[:, cut].astype(f32)
    kv3[...] = kvf[...].reshape(G, NX, 2, HEAD_DIM).astype(bf)

    pl.semaphore_wait(barrier, G * NX - 1 + 4)

    def q_copy(p, t):
        return remote(q3.at[p, t], Q.at[z, x * G + g], sent_sem.at[0], q_sem.at[x], grp=p, blk_1=t)

    def n_copy(p, t):
        return remote(kv3.at[p, t], kvn.at[x * G + g], sent_sem.at[1], n_sem.at[0], grp=p, blk_1=t)

    def landed(ref, sem):
        pltpu.make_async_copy(ref, ref, sem).wait()

    def k_copy(i):
        p = lax.rem(x + i, NX)
        lane = pl.ds(pl.multiple_of(p * HEAD_DIM, HEAD_DIM), HEAD_DIM)
        return remote(ck.at[:, lane], KA.at[rows_from(x), low], sent_sem.at[2], cache_sem.at[0], blk_1=p)

    def v_copy(i):
        p = lax.rem(x + i, NX)
        lane = pl.ds(pl.multiple_of(p * HEAD_DIM, HEAD_DIM), HEAD_DIM)
        return remote(cv.at[:, lane], V.at[rows_from(x)], sent_sem.at[2], cache_sem.at[1], blk_1=p)

    others(lambda p, t: q_copy(p, t).start())
    others(lambda p, t: n_copy(p, t).start())
    loop(1, NX, lambda i: k_copy(i).start())
    loop(1, NX, lambda i: v_copy(i).start())

    Q[z, x * G + g] = q3[g, x]
    kvn[x * G + g] = kv3[g, x]

    for c in ins[5:]:
        c.wait()
    limit = hits[0] - z * N1
    row = lax.broadcasted_iota(jnp.int32, (NK, HEAD_DIM), 0)
    lane0 = lax.broadcasted_iota(jnp.int32, (NK, HEAD_DIM), 1) == 0
    barred = lane0 & (row >= limit) & (row < N1)
    KA[:, HEAD_DIM:] = jnp.where(barred, NEG, 0.0).astype(bf)
    KA[N1:, 0:HEAD_DIM] = jnp.zeros((PN, HEAD_DIM), bf)
    V[N1:, :] = jnp.zeros((PN, HEAD_DIM), bf)
    VT[HEAD_DIM:, :] = jnp.ones((ONES, NK), bf)
    for way in (0, 1):
        for s in range(HX):
            for k in (0, H):
                RB[way, k, s] = jnp.zeros((HEAD_DIM, GR), bf)
                RL[way, k, s] = jnp.full((1, GR), LOWEST, f32)

    def held(way, k):
        return lax.rem(z + (NZ - k if way == 0 else k), NZ)

    def go(way):
        return after if way == 0 else before

    def q_rows(way, k, s):
        return Q.at[held(way, k), pl.ds((way * HX + s) * G, G)]

    def q_on(way, k, s):
        ref = q_rows(way, k, s)
        return remote(ref, ref, sent_sem.at[3], ring_sem.at[way, k, s], blk_0=go(way))

    for s in range(HX):
        for way in (0, 1):
            t = way * HX + s

            @pl.when(x == t)
            def _():
                landed(Q.at[z, pl.ds(t * G, G - 1)], q_sem.at[t])

            @pl.when(x != t)
            def _():
                landed(Q.at[z, pl.ds(t * G, G)], q_sem.at[t])

            q_on(way, 0, s).start()

    def pass_on(k):
        for s in range(HX):
            for way in (0, 1):
                landed(q_rows(way, k, s), ring_sem.at[way, k - 1, s])
                if isinstance(k, int):
                    q_on(way, k, s).start()
                else:
                    pl.when(k < NZ - 1)(lambda way=way, s=s: q_on(way, k, s).start())

    for k in range(1, H):
        pass_on(k)

    landed(kvn.at[pl.ds(0, T - 1)], n_sem.at[0])
    KA[N1 : N1 + T, 0:HEAD_DIM] = kvn[:, 0, :]
    V[N1 : N1 + T, :] = kvn[:, 1, :]
    ins[3].wait()
    landed(V.at[pl.ds(0, (NX - 1) * C)], cache_sem.at[0])

    def position(token, block):
        pos = jnp.full(token.shape, 1 << 20, jnp.int32)
        for s in range(NX):
            here = (token >= s * G) & (token < (s + 1) * G)
            pos = jnp.where(here, assign[block * NX + s] * G + (token - s * G), pos)
        return pos

    first = (lax.broadcasted_iota(jnp.int32, (HR, HEAD_DIM), 1) == 0).astype(f32).astype(bf)

    def scores(k, way, S, M):
        c = held(way, k)
        q = Q[c, pl.ds(way * HX * G, HX * G)].reshape(HR, HEAD_DIM)
        q = jnp.concatenate([q, first], axis=1)
        s = lax.dot_general(KA[...], q, (((1,), (1,)), ((), ())), preferred_element_type=f32)
        pt = position(way * HX * G + lax.broadcasted_iota(jnp.int32, (1, HR), 1) // GROUP, c)
        pu = position(lax.broadcasted_iota(jnp.int32, (PN, 1), 0), z)
        old, new = s[:N1], jnp.where(pu <= pt, s[N1:], NEG)
        S[0:N1] = old
        S[N1:] = new
        M[...] = jnp.maximum(
            jnp.max(old.reshape(N1 // 8, 8, HR), axis=0), jnp.max(new.reshape(PN // 8, 8, HR), axis=0)
        )

    def part_on(way, k, s):
        back = k == H - 1
        slot = jnp.where(back, NZ + 1, k + 1)
        to = jnp.where(back, held(way, k), go(way))
        return (
            remote(SB.at[way, k, s], RB.at[way, slot, s], sent_sem.at[4], part_sem.at[way, k, s], blk_0=to),
            remote(SL.at[way, k, s], RL.at[way, slot, s], sent_sem.at[5], part_sem.at[way, k, s], blk_0=to),
        )

    def part_in(way, k, s):
        landed(size, part_sem.at[way, k - 1, s])

    def blend(k, way, S, M):
        top = jnp.max(M[...], axis=0, keepdims=True)
        p = jnp.exp2((S[...] - top) * TO_LOG2).astype(bf)
        both = jnp.dot(VT[...], p, preferred_element_type=f32)
        weight = both[HEAD_DIM : HEAD_DIM + 1]
        level = top * TO_LOG2 + jnp.log2(weight)
        inverse = 1.0 / weight
        for s in range(HX):
            cut = slice(s * GR, (s + 1) * GR)

            @pl.when((k > 0) & (k != H))
            def _():
                part_in(way, k, s)

            there, here = RL[way, k, s], level[:, cut]
            high = jnp.maximum(there, here)
            a, b = jnp.exp2(there - high), jnp.exp2(here - high)
            both_parts = a + b
            a, b = a / both_parts, b / both_parts * inverse[:, cut]
            merged = RB[way, k, s].astype(f32) * a + both[:HEAD_DIM, cut] * b
            SB[way, k, s] = merged.astype(bf)
            SL[way, k, s] = high + jnp.log2(both_parts)
            for copy in part_on(way, k, s):
                copy.start()

    scores(0, 0, S0, M0)
    ins[4].wait()
    landed(V.at[pl.ds(0, (NX - 1) * C)], cache_sem.at[1])
    VT[0:HEAD_DIM, :] = V[...].T

    def turn(n):
        k = n // 2 + lax.rem(n, 2) * H
        m = jnp.minimum(n + 1, NZ - 1)
        m = m // 2 + lax.rem(m, 2) * H
        scores(k, 1, S1, M1)
        blend(k, 0, S0, M0)

        @pl.when((m >= H) & (n < NZ - 1))
        def _():
            pass_on(m)

        scores(m, 0, S0, M0)
        blend(k, 1, S1, M1)

    loop(0, NZ, turn)

    def o_copy(p, t):
        return remote(res.at[t * G + p], out3.at[g, x], sent_sem.at[6], o_sem.at[0], grp=p, blk_1=t)

    for s in range(HX):
        for way in (0, 1):
            t = way * HX + s
            part_in(way, H, s)
            part_in(way, NZ, s)
            one, two = RL[way, NZ, s], RL[way, NZ + 1, s]
            high = jnp.maximum(one, two)
            a, b = jnp.exp2(one - high), jnp.exp2(two - high)
            done = (RB[way, NZ, s].astype(f32) * a + RB[way, NZ + 1, s].astype(f32) * b) / (a + b)
            done = done.T
            place = assign[z * NX + t] * G + lax.broadcasted_iota(jnp.int32, (GR, 1), 0) // GROUP
            done = jnp.where(place < counts[0], done, 0.0).astype(bf)
            res[t * G : (t + 1) * G] = done.reshape(G, GROUP, HEAD_DIM)

            def give(i, t=t):
                p = peer(i)

                @pl.when((p != g) | (x != t))
                def _():
                    o_copy(p, t).start()

            loop(0, G, give)
    out3[g, x] = res[x * G + g]
    landed(res.at[pl.ds(0, T - 1)], o_sem.at[0])
    wide[...] = out3[...].reshape(G * HEADS, HEAD_DIM).astype(f32)
    for h in range(HEADS):
        out[:, h * HEAD_DIM : (h + 1) * HEAD_DIM] = wide[pl.ds(h, G, stride=HEADS), :].astype(bf)

    landed(res.at[pl.ds(0, T - 1)], sent_sem.at[0])
    landed(kvn.at[pl.ds(0, T - 1)], sent_sem.at[1])
    landed(KA.at[pl.ds(0, (NX - 1) * C)], sent_sem.at[2])
    landed(Q.at[pl.ds(0, NZ - 1), pl.ds(0, 2 * HX * G)], sent_sem.at[3])
    landed(SB, sent_sem.at[4])
    landed(SL, sent_sem.at[5])
    landed(res.at[pl.ds(0, T - 1)], sent_sem.at[6])


def local(queries, cache_keys, cache_values, new_keys, new_values, hits, counts, assign):
    NZ, NX, G = lax.axis_size("blk_0"), lax.axis_size("blk_1"), lax.axis_size("grp")
    C = cache_keys.shape[1]
    T = NX * G
    GR = G * GROUP
    HX = NX // 2
    HR = HX * GR
    N1 = NX * C
    NK = N1 + max(T, 128)
    W = NX * GROUP * HEAD_DIM
    hbm = pl.BlockSpec(memory_space=pltpu.HBM)
    bf, f32 = jnp.bfloat16, jnp.float32
    dma = pltpu.SemaphoreType.DMA
    held = (
        queries.reshape(G, W), new_keys.reshape(G, NX * HEAD_DIM), new_values.reshape(G, NX * HEAD_DIM),
        cache_keys[0], cache_values[0],
    )
    made = pl.pallas_call(
        functools.partial(kernel, G, NZ, NX, C),
        out_shape=jax.ShapeDtypeStruct((G, W), bf),
        in_specs=[hbm] * 8,
        out_specs=pl.BlockSpec(memory_space=pltpu.VMEM),
        scratch_shapes=[
            pltpu.SMEM((1,), jnp.int32),
            pltpu.SMEM((1,), jnp.int32),
            pltpu.SMEM((NZ * NX,), jnp.int32),
            pltpu.VMEM((G, W), bf),
            pltpu.VMEM((G, NX * HEAD_DIM), bf),
            pltpu.VMEM((G, NX * HEAD_DIM), bf),
            pltpu.VMEM((G * NX * GROUP, HEAD_DIM), f32),
            pltpu.VMEM((G, NX, GROUP, HEAD_DIM), bf),
            pltpu.VMEM((G * NX * 2, HEAD_DIM), f32),
            pltpu.VMEM((G, NX, 2, HEAD_DIM), bf),
            pltpu.VMEM((NZ, T, GROUP, HEAD_DIM), bf),
            pltpu.VMEM((NK, 2 * HEAD_DIM), bf),
            pltpu.VMEM((NK, HEAD_DIM), bf),
            pltpu.VMEM((HEAD_DIM + ONES, NK), bf),
            pltpu.VMEM((T, 2, HEAD_DIM), bf),
            pltpu.VMEM((NK, HR), f32),
            pltpu.VMEM((NK, HR), f32),
            pltpu.VMEM((8, HR), f32),
            pltpu.VMEM((8, HR), f32),
            pltpu.VMEM((2, NZ, HX, HEAD_DIM, GR), bf),
            pltpu.VMEM((2, NZ + 2, HX, HEAD_DIM, GR), bf),
            pltpu.VMEM((2, NZ, HX, 1, GR), f32),
            pltpu.VMEM((2, NZ + 2, HX, 1, GR), f32),
            pltpu.VMEM((T, GROUP, HEAD_DIM), bf),
            pltpu.VMEM((G, NX, GROUP, HEAD_DIM), bf),
            pltpu.VMEM((HEAD_DIM // 2 + 1, 1, GR), f32),
            dma((8,)), dma((7,)), dma((NX,)), dma((1,)), dma((2,)),
            dma((2, NZ - 1, HX)), dma((2, NZ, HX)), dma((1,)),
        ],
        compiler_params=pltpu.CompilerParams(
            collective_id=0, has_side_effects=True, vmem_limit_bytes=48 * 1024 * 1024
        ),
        name="attend",
    )(
        *(pltpu.with_memory_space_constraint(a, pltpu.HBM) for a in held), hits, counts,
        pltpu.with_memory_space_constraint(assign[0], pltpu.HBM),
    )
    return made.reshape(G, 1, W)


def solution(mesh):
    finer = Mesh(mesh.devices.reshape(mesh.shape["grp"], 8, 4), ("grp", "blk_0", "blk_1"))
    in_specs = (
        P(None, BLK_GRP, None),
        P("grp", BLK, None),
        P("grp", BLK, None),
        P(None, BLK_GRP, None),
        P(None, BLK_GRP, None),
        P("grp"),
        P("grp"),
        P("grp", None),
    )
    out_specs = P(None, BLK_GRP, None)
    return jax.shard_map(local, mesh=finer, in_specs=in_specs, out_specs=out_specs, check_vma=False)
```

time: 329 us -> 67.4 us (0.20)
  waiting for transfers between devices: 110 us -> 0 us
  Pallas kernels: 0 us -> 65.3 us
  local copies, waits for them, and re-layouts: 58.3 us -> 0.66 us
  blocking collectives: 49.1 us -> 0 us
  other arithmetic: 39 us -> 0 us
  loops' own time: 23.2 us -> 0 us
  matrix products: 16.2 us -> 0 us
  starting transfers between devices: 16.2 us -> 0 us
  between operations: 15.5 us -> 1.3 us
    all_to_all x2 -> x0, waiting for transfers between devices: 75.7 us -> none  [the longest x1 75.7 us: local(): lax.all_to_all(every_out, BLK, split_axis=0, concat_axis=0, tiled=True)]
    pallas_call x0 -> x1, Pallas kernels: none -> 65.3 us  [local(): pl.pallas_call(functools.partial(kernel, G, NZ, NX, C), out_shape=jax.Sha...]
    all_to_all x2 -> x0, blocking collectives: 37.3 us -> none  [the longest x1 18.9 us: side_by_side(): lax.all_to_all(both, axis, split_axis=split_dim, concat_axis=concat_dim,...]
    all_gather x1 -> x0, waiting for transfers between devices: 34.2 us -> none  [gather_axes(): result = lax.all_gather(result, axes[number], axis=dim, tiled=True)]
    another operation x1 -> x0, loops' own time: 23.2 us -> none  [local(): lax.map(one_slice, jnp.arange(kv_heads * part_count, dtype=jnp.int32))]
    all_to_all x2 -> x0, starting transfers between devices: 16.2 us -> none  [the longest x1 9.53 us: local(): lax.all_to_all(every_out, BLK, split_axis=0, concat_axis=0, tiled=True)]
    dot_general x16 -> x0, matrix products: 16.2 us -> none  [the longest x8 9.68 us: partial_block(): jnp.einsum('kgqn,nkd->qkgd', prob_bf, value_heads, preferred_element_type...]
    add x2 -> x0, other arithmetic: 15.3 us -> none  [the longest x1 15.3 us: local(): block_order[every_lane // row_count] * row_count + every_lane % row_count]
  transfers between devices with their start and end apart: 3 -> 0, of which waited for: 2 -> 0; matrix products, arithmetic and copies ran while one was open for 14% -> 0% of each run, Pallas kernels for 0% -> 0%
where the time goes in v2:
time: 67.4 us; the launch traced here: 67.3 us
  Pallas kernels  65.3 us (97%)
  between operations  1.3 us (2%)
    pallas_call x1, Pallas kernels, local(): pl.pallas_call(functools.partial(kernel, G, NZ, NX, C), out_shape=jax.Sha...  65.3 us

profile of v2, /device:TPU:1, one launch (start us, length us, event | category | flops | bytes accessed | tf_op | source)
XLA Modules:
  0.0 67.3 jit_solution(15728146409329149673)
XLA Ops:
  1.3 65.3 %attend.1 = bf16[16,4096]{1,0:T(8,128)(2,1)S(1)} custom-call(bf16[16,4096]{1,0:T(8,128)(2,1)} %bitcast.10, bf16[16,512]{1,0:T(8,128)(2,1)} %bitcast.11, bf16[16,512]{1,0:T(8,128)(2,1)} %bitcast.12, bf16[448,512]{1,0:T(8,128)(2,1)} %bitcast.8, bf16[448,512]{1,0:T(8,128)(2,1)} %bitcast.9, s32[1]{0:T(128)S(6)} %copy.10.hits_hbm, s32[1]{0:T(128)S(6)} %copy.11.counts_hbm, ...), custom_call_target="tpu_custom_call" | custom-call | tf_op jit(solution)/shard_map/attend/pallas_call | solution.py:342
  66.6 0.7 copy.12

commit v3 on v2

--- a/solution.py
+++ b/solution.py
@@ -77,8 +77,8 @@
     after, before = lax.rem(z + 1, NZ), lax.rem(z + NZ - 1, NZ)
     greet(blk_0=after)
     greet(blk_0=before)
-    greet(blk_0=lax.rem(z + H - 1, NZ))
-    greet(blk_0=lax.rem(z + NZ - H + 1, NZ))
+    greet(blk_0=lax.rem(z + 2, NZ))
+    greet(blk_0=lax.rem(z + NZ - 2, NZ))
 
     own_lane = pl.ds(pl.multiple_of(x * HEAD_DIM, HEAD_DIM), HEAD_DIM)
     low = pl.ds(0, HEAD_DIM)
@@ -133,8 +133,8 @@
         return remote(cv.at[:, lane], V.at[rows_from(x)], sent_sem.at[2], cache_sem.at[1], blk_1=p)
 
     others(lambda p, t: q_copy(p, t).start())
+    loop(1, NX, lambda i: k_copy(i).start())
     others(lambda p, t: n_copy(p, t).start())
-    loop(1, NX, lambda i: k_copy(i).start())
     loop(1, NX, lambda i: v_copy(i).start())
 
     Q[z, x * G + g] = q3[g, x]
@@ -152,9 +152,8 @@
     VT[HEAD_DIM:, :] = jnp.ones((ONES, NK), bf)
     for way in (0, 1):
         for s in range(HX):
-            for k in (0, H):
-                RB[way, k, s] = jnp.zeros((HEAD_DIM, GR), bf)
-                RL[way, k, s] = jnp.full((1, GR), LOWEST, f32)
+            RB[way, NZ + 1, s] = jnp.zeros((HEAD_DIM, GR), bf)
+            RL[way, NZ + 1, s] = jnp.full((1, GR), LOWEST, f32)
 
     def held(way, k):
         return lax.rem(z + (NZ - k if way == 0 else k), NZ)
@@ -165,9 +164,13 @@
     def q_rows(way, k, s):
         return Q.at[held(way, k), pl.ds((way * HX + s) * G, G)]
 
-    def q_on(way, k, s):
+    routes = {0: (2, 1), 2: (4, 3), 4: (5,), 5: (6,), 6: (7,)} if NZ == 8 else {0: (2, 1), 2: (3,)}
+    due = {4: (4,), 3: (3,), 5: (5,), 6: (6,), 1: (1,), 7: (7,)} if NZ == 8 else {2: (2,), 1: (1,), 3: (3,)}
+
+    def q_on(way, k, s, hop):
         ref = q_rows(way, k, s)
-        return remote(ref, ref, sent_sem.at[3], ring_sem.at[way, k, s], blk_0=go(way))
+        to = lax.rem(z + (hop if way == 0 else NZ - hop), NZ)
+        return remote(ref, ref, sent_sem.at[3], ring_sem.at[way, k + hop - 1, s], blk_0=to)
 
     for s in range(HX):
         for way in (0, 1):
@@ -181,19 +184,24 @@
             def _():
                 landed(Q.at[z, pl.ds(t * G, G)], q_sem.at[t])
 
-            q_on(way, 0, s).start()
+            q_on(way, 0, s, 2).start()
 
     def pass_on(k):
         for s in range(HX):
             for way in (0, 1):
                 landed(q_rows(way, k, s), ring_sem.at[way, k - 1, s])
-                if isinstance(k, int):
-                    q_on(way, k, s).start()
-                else:
-                    pl.when(k < NZ - 1)(lambda way=way, s=s: q_on(way, k, s).start())
-
-    for k in range(1, H):
+                for further in routes.get(k, ())[:1]:
+                    q_on(way, k, s, further - k).start()
+        for further in routes.get(k, ())[1:]:
+            for s in range(HX):
+                for way in (0, 1):
+                    q_on(way, k, s, further - k).start()
+
+    for k in range(2, H, 2):
         pass_on(k)
+    for s in range(HX):
+        for way in (0, 1):
+            q_on(way, 0, s, 1).start()
 
     landed(kvn.at[pl.ds(0, T - 1)], n_sem.at[0])
     KA[N1 : N1 + T, 0:HEAD_DIM] = kvn[:, 0, :]
@@ -225,16 +233,15 @@
         )
 
     def part_on(way, k, s):
-        back = k == H - 1
-        slot = jnp.where(back, NZ + 1, k + 1)
-        to = jnp.where(back, held(way, k), go(way))
+        slot = jnp.where(k >= H, k + 1, k - 1)
+        to = jnp.where(k >= H, go(way), go(1 - way))
         return (
-            remote(SB.at[way, k, s], RB.at[way, slot, s], sent_sem.at[4], part_sem.at[way, k, s], blk_0=to),
-            remote(SL.at[way, k, s], RL.at[way, slot, s], sent_sem.at[5], part_sem.at[way, k, s], blk_0=to),
+            remote(SB.at[way, k, s], RB.at[way, slot, s], sent_sem.at[4], part_sem.at[way, slot, s], blk_0=to),
+            remote(SL.at[way, k, s], RL.at[way, slot, s], sent_sem.at[5], part_sem.at[way, slot, s], blk_0=to),
         )
 
-    def part_in(way, k, s):
-        landed(size, part_sem.at[way, k - 1, s])
+    def part_in(way, slot, s):
+        landed(size, part_sem.at[way, slot, s])
 
     def blend(k, way, S, M):
         top = jnp.max(M[...], axis=0, keepdims=True)
@@ -243,39 +250,47 @@
         weight = both[HEAD_DIM : HEAD_DIM + 1]
         level = top * TO_LOG2 + jnp.log2(weight)
         inverse = 1.0 / weight
+        fresh = (k == 0) | (k == H - 1) | (k == H)
+        slot = jnp.where(fresh, NZ + 1, k)
         for s in range(HX):
             cut = slice(s * GR, (s + 1) * GR)
 
-            @pl.when((k > 0) & (k != H))
+            @pl.when(jnp.logical_not(fresh))
             def _():
                 part_in(way, k, s)
 
-            there, here = RL[way, k, s], level[:, cut]
+            there, here = RL[way, slot, s], level[:, cut]
             high = jnp.maximum(there, here)
             a, b = jnp.exp2(there - high), jnp.exp2(here - high)
             both_parts = a + b
             a, b = a / both_parts, b / both_parts * inverse[:, cut]
-            merged = RB[way, k, s].astype(f32) * a + both[:HEAD_DIM, cut] * b
+            merged = RB[way, slot, s].astype(f32) * a + both[:HEAD_DIM, cut] * b
             SB[way, k, s] = merged.astype(bf)
             SL[way, k, s] = high + jnp.log2(both_parts)
-            for copy in part_on(way, k, s):
-                copy.start()
+
+            @pl.when(k > 0)
+            def _():
+                for copy in part_on(way, k, s):
+                    copy.start()
 
     scores(0, 0, S0, M0)
     ins[4].wait()
     landed(V.at[pl.ds(0, (NX - 1) * C)], cache_sem.at[1])
     VT[0:HEAD_DIM, :] = V[...].T
 
+    def step_of(n):
+        return jnp.where(lax.rem(n, 2) == 1, H + n // 2, jnp.where(n == 0, 0, H - n // 2))
+
     def turn(n):
-        k = n // 2 + lax.rem(n, 2) * H
-        m = jnp.minimum(n + 1, NZ - 1)
-        m = m // 2 + lax.rem(m, 2) * H
+        k, m = step_of(n), step_of(jnp.minimum(n + 1, NZ - 1))
         scores(k, 1, S1, M1)
         blend(k, 0, S0, M0)
-
-        @pl.when((m >= H) & (n < NZ - 1))
-        def _():
-            pass_on(m)
+        for at, steps in due.items():
+
+            @pl.when((m == at) & (n < NZ - 1))
+            def _():
+                for step in steps:
+                    pass_on(step)
 
         scores(m, 0, S0, M0)
         blend(k, 1, S1, M1)
@@ -288,12 +303,13 @@
     for s in range(HX):
         for way in (0, 1):
             t = way * HX + s
-            part_in(way, H, s)
+            part_in(way, 0, s)
             part_in(way, NZ, s)
-            one, two = RL[way, NZ, s], RL[way, NZ + 1, s]
-            high = jnp.maximum(one, two)
-            a, b = jnp.exp2(one - high), jnp.exp2(two - high)
-            done = (RB[way, NZ, s].astype(f32) * a + RB[way, NZ + 1, s].astype(f32) * b) / (a + b)
+            one, two, own = RL[way, 0, s], RL[way, NZ, s], SL[way, 0, s]
+            high = jnp.maximum(jnp.maximum(one, two), own)
+            a, b, c = jnp.exp2(one - high), jnp.exp2(two - high), jnp.exp2(own - high)
+            done = RB[way, 0, s].astype(f32) * a + RB[way, NZ, s].astype(f32) * b
+            done = (done + SB[way, 0, s].astype(f32) * c) / (a + b + c)
             done = done.T
             place = assign[z * NX + t] * G + lax.broadcasted_iota(jnp.int32, (GR, 1), 0) // GROUP
             done = jnp.where(place < counts[0], done, 0.0).astype(bf)
@@ -317,8 +333,8 @@
     landed(kvn.at[pl.ds(0, T - 1)], sent_sem.at[1])
     landed(KA.at[pl.ds(0, (NX - 1) * C)], sent_sem.at[2])
     landed(Q.at[pl.ds(0, NZ - 1), pl.ds(0, 2 * HX * G)], sent_sem.at[3])
-    landed(SB, sent_sem.at[4])
-    landed(SL, sent_sem.at[5])
+    landed(SB.at[:, pl.ds(1, NZ - 1)], sent_sem.at[4])
+    landed(SL.at[:, pl.ds(1, NZ - 1)], sent_sem.at[5])
     landed(res.at[pl.ds(0, T - 1)], sent_sem.at[6])
 
 
@@ -372,7 +388,7 @@
             pltpu.VMEM((G, NX, GROUP, HEAD_DIM), bf),
             pltpu.VMEM((HEAD_DIM // 2 + 1, 1, GR), f32),
             dma((8,)), dma((7,)), dma((NX,)), dma((1,)), dma((2,)),
-            dma((2, NZ - 1, HX)), dma((2, NZ, HX)), dma((1,)),
+            dma((2, NZ - 1, HX)), dma((2, NZ + 1, HX)), dma((1,)),
         ],
         compiler_params=pltpu.CompilerParams(
             collective_id=0, has_side_effects=True, vmem_limit_bytes=48 * 1024 * 1024

time: 67.4 us -> 61.5 us (0.912)
  Pallas kernels: 65.3 us -> 59.4 us
    pallas_call x1, Pallas kernels: 65.3 us -> 59.4 us  [local(): pl.pallas_call(functools.partial(kernel, G, NZ, NX, C), out_shape=jax.Sha...]
where the time goes in v3:
time: 61.5 us; the launch traced here: 61.3 us
  Pallas kernels  59.4 us (97%)
  between operations  1.3 us (2%)
  local copies, waits for them, and re-layouts  0.66 us (1%)
    pallas_call x1, Pallas kernels, local(): pl.pallas_call(functools.partial(kernel, G, NZ, NX, C), out_shape=jax.Sha...  59.4 us

profile of v3, /device:TPU:1, one launch (start us, length us, event | category | flops | bytes accessed | tf_op | source)
XLA Modules:
  0.0 61.3 jit_solution(117179280890522691)
XLA Ops:
  1.3 59.4 %attend.1 = bf16[16,4096]{1,0:T(8,128)(2,1)S(1)} custom-call(bf16[16,4096]{1,0:T(8,128)(2,1)} %bitcast.10, bf16[16,512]{1,0:T(8,128)(2,1)} %bitcast.11, bf16[16,512]{1,0:T(8,128)(2,1)} %bitcast.12, bf16[448,512]{1,0:T(8,128)(2,1)} %bitcast.8, bf16[448,512]{1,0:T(8,128)(2,1)} %bitcast.9, s32[1]{0:T(128)S(6)} %copy.10.hits_hbm, s32[1]{0:T(128)S(6)} %copy.11.counts_hbm, ...), custom_call_target="tpu_custom_call" | custom-call | tf_op jit(solution)/shard_map/attend/pallas_call | solution.py:358
  60.7 0.7 %copy.12 = bf16[16,1,4096]{2,0,1:T(8,128)(2,1)} copy(bf16[16,1,4096]{2,0,1:T(8,128)(2,1)S(1)} %bitcast.7) | data formatting | bytes 262144

commit v4 on v3

--- a/solution.py
+++ b/solution.py
@@ -53,18 +53,18 @@
 
     def peer(i):
         k = i // 2
-        far = jnp.where(k == 0, Y // 2, (Y - k) // 2)
-        step = jnp.where(lax.rem(k, 2) == 1, far, Y - far)
+        far = Y // 2 if k == 0 else (Y - k) // 2
+        step = far if k % 2 == 1 else Y - far
         return lax.rem(g // 2 + step, Y) * 2 + lax.rem(g + 1 + i, 2)
 
     turns = [lax.rem(x + 1 + j, NX) for j in range(NX)]
 
+    peers = [peer(i) for i in range(G - 1)]
+
     def others(fn):
-        def one(i):
-            p = peer(i)
+        for p in peers:
             for t in turns:
                 fn(p, t)
-        loop(0, G - 1, one)
         for t in turns[:-1]:
             fn(g, t)
 
@@ -165,7 +165,7 @@
         return Q.at[held(way, k), pl.ds((way * HX + s) * G, G)]
 
     routes = {0: (2, 1), 2: (4, 3), 4: (5,), 5: (6,), 6: (7,)} if NZ == 8 else {0: (2, 1), 2: (3,)}
-    due = {4: (4,), 3: (3,), 5: (5,), 6: (6,), 1: (1,), 7: (7,)} if NZ == 8 else {2: (2,), 1: (1,), 3: (3,)}
+    due = {3: (3,), 5: (5,), 6: (6,), 1: (1,), 7: (7,)} if NZ == 8 else {1: (1,), 3: (3,)}
 
     def q_on(way, k, s, hop):
         ref = q_rows(way, k, s)
@@ -246,7 +246,8 @@
     def blend(k, way, S, M):
         top = jnp.max(M[...], axis=0, keepdims=True)
         p = jnp.exp2((S[...] - top) * TO_LOG2).astype(bf)
-        both = jnp.dot(VT[...], p, preferred_element_type=f32)
+        both = jnp.dot(VT[:, :N1], p[:N1], preferred_element_type=f32)
+        both = both + jnp.dot(VT[:, N1:], p[N1:], preferred_element_type=f32)
         weight = both[HEAD_DIM : HEAD_DIM + 1]
         level = top * TO_LOG2 + jnp.log2(weight)
         inverse = 1.0 / weight
@@ -273,13 +274,14 @@
                 for copy in part_on(way, k, s):
                     copy.start()
 
-    scores(0, 0, S0, M0)
+    pass_on(H)
+    scores(H, 0, S0, M0)
     ins[4].wait()
     landed(V.at[pl.ds(0, (NX - 1) * C)], cache_sem.at[1])
     VT[0:HEAD_DIM, :] = V[...].T
 
     def step_of(n):
-        return jnp.where(lax.rem(n, 2) == 1, H + n // 2, jnp.where(n == 0, 0, H - n // 2))
+        return jnp.where(lax.rem(n, 2) == 0, H + n // 2, H - 1 - n // 2)
 
     def turn(n):
         k, m = step_of(n), step_of(jnp.minimum(n + 1, NZ - 1))
@@ -315,14 +317,9 @@
             done = jnp.where(place < counts[0], done, 0.0).astype(bf)
             res[t * G : (t + 1) * G] = done.reshape(G, GROUP, HEAD_DIM)
 
-            def give(i, t=t):
-                p = peer(i)
-
-                @pl.when((p != g) | (x != t))
-                def _():
-                    o_copy(p, t).start()
-
-            loop(0, G, give)
+            for p in peers:
+                o_copy(p, t).start()
+            pl.when(x != t)(lambda t=t: o_copy(g, t).start())
     out3[g, x] = res[x * G + g]
     landed(res.at[pl.ds(0, T - 1)], o_sem.at[0])
     wide[...] = out3[...].reshape(G * HEADS, HEAD_DIM).astype(f32)

time: 61.5 us -> 61.7 us (level)
  no operation moved by 1% of the time
where the time goes in v4:
time: 61.7 us; the launch traced here: 61.5 us
  Pallas kernels  59.6 us (97%)
  between operations  1.3 us (2%)
  local copies, waits for them, and re-layouts  0.66 us (1%)
    pallas_call x1, Pallas kernels, local(): pl.pallas_call(functools.partial(kernel, G, NZ, NX, C), out_shape=jax.Sha...  59.6 us

profile of v4, /device:TPU:1, one launch (start us, length us, event | category | flops | bytes accessed | tf_op | source)
XLA Modules:
  0.0 61.5 jit_solution(13465814035031358500)
XLA Ops:
  1.3 59.6 %attend.1 = bf16[16,4096]{1,0:T(8,128)(2,1)S(1)} custom-call(bf16[16,4096]{1,0:T(8,128)(2,1)} %bitcast.10, bf16[16,512]{1,0:T(8,128)(2,1)} %bitcast.11, bf16[16,512]{1,0:T(8,128)(2,1)} %bitcast.12, bf16[448,512]{1,0:T(8,128)(2,1)} %bitcast.8, bf16[448,512]{1,0:T(8,128)(2,1)} %bitcast.9, s32[1]{0:T(128)S(6)} %copy.10.hits_hbm, s32[1]{0:T(128)S(6)} %copy.11.counts_hbm, ...), custom_call_target="tpu_custom_call" | custom-call | tf_op jit(solution)/shard_map/attend/pallas_call | solution.py:355
  60.9 0.7 %copy.12 = bf16[16,1,4096]{2,0,1:T(8,128)(2,1)} copy(bf16[16,1,4096]{2,0,1:T(8,128)(2,1)S(1)} %bitcast.7) | data formatting | bytes 262144
